TPU v7x, 32 devices: a whole 2x2x4 slice. The times are simulated.
32 devices in a mesh: row: 8 (over z, x), col: 4 (over y, core).
Axes of the slice: x: 2, y: 2, z: 4, core: 2. Of those that a mesh axis runs over, the one named last changes fastest.
Arguments:
- tokens: bfloat16 [512, 12288], P('col', 'row'), may hold values from -16 to 16
- norm_gain: float32 [12288], P('row'), may hold values from 0.25 to 1.75
- weight_in: bfloat16 [12288, 49152], P('row', 'col'), may hold values from -0.0546875 to 0.0546875
- weight_out: bfloat16 [49152, 12288], P('col', 'row'), may hold values from -0.02734375 to 0.02734375
Outputs:
- mixed: bfloat16 [512, 12288], P('col', 'row')
All inputs are finite; a program needn't handle non-finite values.
Results may differ from a plain program's by a relative error of at most 0.0051.
Values may be sent and summed in bfloat16 or wider, within the bound.
A program may use at most 192 MiB of HBM per device.

v0:
```python
import jax
import jax.numpy as jnp
from jax import lax
from jax.sharding import PartitionSpec as P

D = 12288


epsilon = 1e-05


def per_device(tokens, norm_gain, weight_in, weight_out):
    gathered = lax.all_gather(tokens, "col", axis=0, tiled=True)
    wide_input = gathered.astype(jnp.float32)
    scaled = (wide_input * norm_gain[None, :]).astype(jnp.bfloat16)
    squares = jnp.sum(wide_input * wide_input, axis=1)
    partial_value = jnp.dot(scaled, weight_in, preferred_element_type=jnp.float32)
    hidden_sum, square_sum = (
        lax.psum_scatter(partial_value, "row", scatter_dimension=0, tiled=True),
        lax.psum_scatter(squares, "row", scatter_dimension=0, tiled=True),
    )
    inverse = lax.rsqrt(square_sum / D + epsilon)
    hidden = hidden_sum * inverse[:, None]
    active = jax.nn.gelu(hidden, approximate=True).astype(jnp.bfloat16)
    branch = jnp.dot(
        lax.all_gather(active, "row", axis=0, tiled=True),
        weight_out,
        preferred_element_type=jnp.float32,
    )
    output_rows = lax.psum_scatter(branch, "col", scatter_dimension=0, tiled=True)
    return (tokens.astype(jnp.float32) + output_rows).astype(jnp.bfloat16)


def solution(mesh):
    in_specs = (P("col", "row"), P("row"), P("row", "col"), P("col", "row"))
    out_specs = P("col", "row")
    return jax.shard_map(
        per_device, mesh=mesh, in_specs=in_specs, out_specs=out_specs, check_vma=False
    )
```

profile of v0, /device:TPU:0, one launch (start us, length us, event | category | flops | bytes accessed | tf_op | source)
XLA Modules:
  0.0 716.1 jit_solution(16576119395033260583)
XLA Ops:
  6.5 0.0 all-gather.3.cloned.1.call-start
  6.5 0.7 all-gather.3.cloned.1.call-update
  7.3 0.0 reduce-scatter.3.cloned.1.call-start
  7.3 24.0 %all-gather.3.cloned.1.call-done = bf16[512,1536]{1,0:T(8,128)(2,1)} async-done(((bf16[128,1536]{1,0:T(8,128)(2,1)}), bf16[512,1536]{1,0:T(8,128)(2,1)}) %all-gather.3.cloned.1.call-update) | async-done | bytes 1572880 | tf_op jit(solution)/shard_map/all_gather | solution.py:13
  31.3 29.4 %fusion.10 = f32[512,12288]{1,0:T(8,128)} fusion(bf16[1536,12288]{1,0:T(8,128)(2,1)} %param.6, bf16[512,1536]{1,0:T(8,128)(2,1)} %all-gather.3.cloned.1.call-done, f32[1536]{0:T(1024)} %param.5), kind=kOutput, calls=%fused_computation.13 | convolution fusion | flops 19329712128 | bytes 64493568 | tf_op jit(solution)/shard_map/dot_general | solution.py:17
  60.7 0.0 copy-start.2
  60.7 0.0 copy-start
  60.7 0.0 reduce-scatter.3.cloned.1.call-update
  60.7 0.0 all-gather.5.cloned.1.call-start
  60.8 0.6 copy-done.2
  61.4 0.6 dynamic-slice
  62.6 0.0 copy-done
  62.6 0.4 fusion.1
  63.0 22.7 %all-reduce = f32[512]{0:T(512)S(1)} all-reduce(f32[512]{0:T(512)S(1)} %fusion.1), channel_id=3, replica_groups=mesh['row'=8,'col'=4] {'row'}, use_global_device_ids=true, to_apply=%region_2.0.clone | all-reduce | flops 512 | bytes 4096
  85.6 0.1 fusion.14
  85.7 378.6 %reduce-scatter.3.cloned.1.call-done = f32[64,12288]{1,0:T(8,128)} async-done(((f32[512,12288]{1,0:T(8,128)}), f32[64,12288]{1,0:T(8,128)}) %reduce-scatter.3.cloned.1.call-update) | async-done | bytes 3145744 | tf_op jit(solution)/shard_map/reduce_scatter | solution.py:19
  464.4 4.2 fusion.9
  468.6 0.0 all-gather.5.cloned.1.call-update
  468.6 0.0 reduce-scatter.5.cloned.1.call-start
  468.7 175.3 %all-gather.5.cloned.1.call-done = bf16[512,12288]{1,0:T(8,128)(2,1)} async-done(((bf16[64,12288]{1,0:T(8,128)(2,1)}), bf16[512,12288]{1,0:T(8,128)(2,1)}) %all-gather.5.cloned.1.call-update) | async-done | bytes 12582928 | tf_op jit(solution)/shard_map/all_gather | solution.py:26
  644.0 27.5 %fusion.15 = f32[512,1536]{1,0:T(8,128)} fusion(bf16[512,12288]{1,0:T(8,128)(2,1)} %all-gather.5.cloned.1.call-done, bf16[12288,1536]{1,0:T(8,128)(2,1)} %param.7), kind=kOutput, calls=%fused_computation.19 | convolution fusion | flops 19327352832 | bytes 53477376 | tf_op jit(solution)/shard_map/dot_general | solution.py:25
  671.4 0.0 copy-start.1
  671.4 0.0 reduce-scatter.5.cloned.1.call-update
  671.4 36.2 %reduce-scatter.5.cloned.1.call-done = f32[128,1536]{1,0:T(8,128)} async-done(((f32[512,1536]{1,0:T(8,128)}), f32[128,1536]{1,0:T(8,128)}) %reduce-scatter.5.cloned.1.call-update) | async-done | bytes 786448 | tf_op jit(solution)/shard_map/reduce_scatter | solution.py:30
  707.7 0.0 copy-done.1
  707.7 1.9 add_convert_fusion
Async XLA Ops:
  6.5 24.7 %all-gather.3.cloned.1.call-start = ((), (), s32[]{:S(2)}) async-start(), calls=%async_computation.2 | async-start | bytes 1966080 | tf_op jit(solution)/shard_map/all_gather | solution.py:13
  7.3 457.1 %reduce-scatter.3.cloned.1.call-start = ((), (), s32[]{:S(2)}) async-start(), calls=%async_computation.3 | async-start | bytes 28311552 | tf_op jit(solution)/shard_map/reduce_scatter | solution.py:19
  60.7 0.7 copy-start.2
  60.7 1.9 copy-start
  60.7 583.2 %all-gather.5.cloned.1.call-start = ((), (), s32[]{:S(2)}) async-start(), calls=%async_computation.4 | async-start | bytes 14155776 | tf_op jit(solution)/shard_map/all_gather | solution.py:26
  468.6 239.1 %reduce-scatter.5.cloned.1.call-start = ((), (), s32[]{:S(2)}) async-start(), calls=%async_computation.5 | async-start | bytes 3932160 | tf_op jit(solution)/shard_map/reduce_scatter | solution.py:30
  671.4 36.2 %copy-start.1 = (bf16[128,1536]{1,0:T(8,128)(2,1)S(1)}, bf16[128,1536]{1,0:T(8,128)(2,1)}, u32[]{:S(2)}) copy-start(bf16[128,1536]{1,0:T(8,128)(2,1)} %param.4) | copy-start | bytes 1179652
Sparse Core Ops, SparseCore 0:
  8.9 22.3 all-gather.2
  60.9 403.4 reduce-scatter.2
  468.7 175.1 all-gather.4
  671.6 36.0 reduce-scatter.4
where the time goes:
time: 716 us
  waiting for transfers between devices  615 us (86%)
  matrix products  56.9 us (8%)
  blocking collectives  22.7 us (3%)
  between operations  13.8 us (2%)
    reduce_scatter x1, waiting for transfers between devices, per_device(): lax.psum_scatter(partial_value, 'row', scatter_dimension=0, tiled=True)  379 us
    all_gather x1, waiting for transfers between devices, per_device(): lax.all_gather(active, 'row', axis=0, tiled=True)  175 us
    reduce_scatter x1, waiting for transfers between devices, per_device(): lax.psum_scatter(branch, 'col', scatter_dimension=0, tiled=True)  36.2 us
    dot_general x1, matrix products, per_device(): jnp.dot(scaled, weight_in, preferred_element_type=jnp.float32)  29.4 us
    dot_general x1, matrix products, per_device(): jnp.dot(lax.all_gather(active, 'row', axis=0, tiled=True), weight_out, pr...  27.5 us
    all_gather x1, waiting for transfers between devices, per_device(): gathered = lax.all_gather(tokens, 'col', axis=0, tiled=True)  24 us
    unnamed x1, blocking collectives  22.7 us
  transfers between devices with their start and end apart: 4, of which 4 were waited for; matrix products, arithmetic and copies ran while one was open for 0% of the time, Pallas kernels for 0%

commit v1 on v0

v1 whole, which is shorter than its diff:
```python
import jax
import jax.numpy as jnp
from jax import lax
from jax.sharding import PartitionSpec as P

epsilon = 1e-05


def make(mesh):
    rows = mesh.shape["row"]

    def per_device(tokens, norm_gain, weight_in, weight_out):
        width = weight_in.shape[0] * rows
        gathered = lax.all_gather(tokens, "col", axis=0, tiled=True)
        wide_input = gathered.astype(jnp.float32)
        scaled = (wide_input * norm_gain[None, :]).astype(jnp.bfloat16)
        squares = jnp.sum(wide_input * wide_input, axis=1)
        square_sum = squares
        for shift in range(1, rows):
            square_sum = square_sum + lax.ppermute(
                squares, "row", [(i, (i + shift) % rows) for i in range(rows)]
            )
        own = squares.shape[0] // rows
        square_sum = lax.dynamic_slice_in_dim(
            square_sum, lax.axis_index("row") * own, own
        )
        partial_value = jnp.dot(
            scaled, weight_in, preferred_element_type=jnp.float32
        ).astype(jnp.bfloat16)
        hidden_sum = lax.psum_scatter(
            partial_value, "row", scatter_dimension=0, tiled=True
        ).astype(jnp.float32)
        inverse = lax.rsqrt(square_sum / width + epsilon)
        hidden = hidden_sum * inverse[:, None]
        active = jax.nn.gelu(hidden, approximate=True).astype(jnp.bfloat16)
        branch = jnp.dot(
            lax.all_gather(active, "row", axis=0, tiled=True),
            weight_out,
            preferred_element_type=jnp.float32,
        ).astype(jnp.bfloat16)
        output_rows = lax.psum_scatter(
            branch, "col", scatter_dimension=0, tiled=True
        ).astype(jnp.float32)
        return (tokens.astype(jnp.float32) + output_rows).astype(jnp.bfloat16)

    return per_device


def solution(mesh):
    in_specs = (P("col", "row"), P("row"), P("row", "col"), P("col", "row"))
    out_specs = P("col", "row")
    return jax.shard_map(
        make(mesh), mesh=mesh, in_specs=in_specs, out_specs=out_specs, check_vma=False
    )
```

time: 716 us -> 508 us (0.71)
  waiting for transfers between devices: 615 us -> 422 us
  blocking collectives: 22.7 us -> 0 us
  starting transfers between devices: 0.12 us -> 10.8 us
    reduce_scatter x1, waiting for transfers between devices: 379 us -> 190 us  [per_device(): lax.psum_scatter(partial_value, 'row', scatter_dimension=0, tiled=True)]
    unnamed x1 -> x0, blocking collectives: 22.7 us -> none
    ppermute x0 -> x7, starting transfers between devices: none -> 10.7 us  [per_device(): lax.ppermute(squares, 'row', [(i, (i + shift) % rows) for i in range(rows)])]
    reduce_scatter x1, waiting for transfers between devices: 36.2 us -> 26.4 us  [per_device(): lax.psum_scatter(branch, 'col', scatter_dimension=0, tiled=True)]
  transfers between devices with their start and end apart: 4 -> 11, of which waited for: 4 -> 7; matrix products, arithmetic and copies ran while one was open for 0% -> 0% of each run, Pallas kernels for 0% -> 0%
where the time goes in v1:
time: 508 us; the launch traced here: 507 us
  waiting for transfers between devices  422 us (83%)
  matrix products  54.3 us (11%)
  between operations  13.1 us (3%)
  starting transfers between devices  10.8 us (2%)
  other arithmetic  6.09 us (1%)
    reduce_scatter x1, waiting for transfers between devices, per_device(): lax.psum_scatter(partial_value, 'row', scatter_dimension=0, tiled=True)  190 us
    all_gather x1, waiting for transfers between devices, per_device(): lax.all_gather(active, 'row', axis=0, tiled=True)  175 us
    dot_general x1, matrix products, per_device(): jnp.dot(scaled, weight_in, preferred_element_type=jnp.float32)  27.2 us
    dot_general x1, matrix products, per_device(): jnp.dot(lax.all_gather(active, 'row', axis=0, tiled=True), weight_out, pr...  27.2 us
    reduce_scatter x1, waiting for transfers between devices, per_device(): lax.psum_scatter(branch, 'col', scatter_dimension=0, tiled=True)  26.4 us
    all_gather x1, waiting for transfers between devices, per_device(): gathered = lax.all_gather(tokens, 'col', axis=0, tiled=True)  24 us
    ppermute x7, starting transfers between devices, per_device(): lax.ppermute(squares, 'row', [(i, (i + shift) % rows) for i in range(rows)])  10.7 us
  transfers between devices with their start and end apart: 11, of which 7 were waited for; matrix products, arithmetic and copies ran while one was open for 0% of the time, Pallas kernels for 0%

profile of v1, /device:TPU:0, one launch (start us, length us, event | category | flops | bytes accessed | tf_op | source)
XLA Modules:
  0.0 507.4 jit_solution(16543680506113687024)
XLA Ops:
  6.5 0.0 all-gather.3.cloned.1.call-start
  6.5 0.7 all-gather.3.cloned.1.call-update
  7.3 0.0 reduce-scatter.3.cloned.1.call-start
  7.3 24.0 %all-gather.3.cloned.1.call-done = bf16[512,1536]{1,0:T(8,128)(2,1)} async-done(((bf16[128,1536]{1,0:T(8,128)(2,1)}), bf16[512,1536]{1,0:T(8,128)(2,1)}) %all-gather.3.cloned.1.call-update) | async-done | bytes 1572880 | tf_op jit(solution)/shard_map/all_gather | solution.py:14
  31.3 27.2 %convolution_convert_fusion = bf16[512,12288]{1,0:T(8,128)(2,1)} fusion(bf16[1536,12288]{1,0:T(8,128)(2,1)} %param.6, bf16[512,1536]{1,0:T(8,128)(2,1)} %all-gather.3.cloned.1.call-done, f32[1536]{0:T(1024)} %param.5), kind=kOutput, calls=%fused_computation | convolution fusion | flops 19336003584 | bytes 51910656 | tf_op jit(solution)/shard_map/dot_general | solution.py:27
  58.5 0.0 copy-start
  58.5 0.0 reduce-scatter.3.cloned.1.call-update
  58.5 0.0 all-gather.5.cloned.1.call-start
  58.5 1.3 copy-done
  59.9 0.4 fusion.1
  60.2 4.3 collective-permute-start.6
  64.5 0.5 collective-permute-start.5
  65.1 0.0 collective-permute-start.4
  65.1 2.9 collective-permute-start.3
  68.0 0.0 collective-permute-start.2
  68.0 0.0 collective-permute-done.6
  68.0 2.0 collective-permute-start.1
  70.0 0.0 collective-permute-done.5
  70.0 0.9 collective-permute-start
  70.9 0.0 collective-permute-done.4
  71.0 0.0 collective-permute-done.3
  71.0 2.6 collective-permute-done.2
  73.6 1.1 collective-permute-done.1
  74.6 1.9 collective-permute-done
  76.5 0.1 add_rsqrt_fusion
  76.6 189.6 %reduce-scatter.3.cloned.1.call-done = bf16[64,12288]{1,0:T(8,128)(2,1)} async-done(((bf16[512,12288]{1,0:T(8,128)(2,1)}), bf16[64,12288]{1,0:T(8,128)(2,1)}) %reduce-scatter.3.cloned.1.call-update) | async-done | bytes 1572880 | tf_op jit(solution)/shard_map/reduce_scatter | solution.py:30
  266.2 3.8 fusion.9
  270.0 0.0 all-gather.5.cloned.1.call-update
  270.0 0.0 copy-start.1
  270.1 0.0 reduce-scatter.5.cloned.1.call-start
  270.1 175.3 %all-gather.5.cloned.1.call-done = bf16[512,12288]{1,0:T(8,128)(2,1)} async-done(((bf16[64,12288]{1,0:T(8,128)(2,1)}), bf16[512,12288]{1,0:T(8,128)(2,1)}) %all-gather.5.cloned.1.call-update) | async-done | bytes 12582928 | tf_op jit(solution)/shard_map/all_gather | solution.py:37
  445.4 27.2 %convolution_convert_fusion.1 = bf16[512,1536]{1,0:T(8,128)(2,1)} fusion(bf16[512,12288]{1,0:T(8,128)(2,1)} %all-gather.5.cloned.1.call-done, bf16[12288,1536]{1,0:T(8,128)(2,1)} %param.7), kind=kOutput, calls=%fused_computation.14 | convolution fusion | flops 19328139264 | bytes 51904512 | tf_op jit(solution)/shard_map/dot_general | solution.py:36
  472.6 0.0 reduce-scatter.5.cloned.1.call-update
  472.6 26.4 %reduce-scatter.5.cloned.1.call-done = bf16[128,1536]{1,0:T(8,128)(2,1)} async-done(((bf16[512,1536]{1,0:T(8,128)(2,1)}), bf16[128,1536]{1,0:T(8,128)(2,1)}) %reduce-scatter.5.cloned.1.call-update) | async-done | bytes 393232 | tf_op jit(solution)/shard_map/reduce_scatter | solution.py:41
  499.0 0.0 copy-done.1
  499.0 1.8 add_convert_fusion
  (1 shorter events, 0.0 us)
Async XLA Ops:
  6.5 24.7 %all-gather.3.cloned.1.call-start = ((), (), s32[]{:S(2)}) async-start(), calls=%async_computation.2 | async-start | bytes 1966080 | tf_op jit(solution)/shard_map/all_gather | solution.py:14
  7.3 259.0 %reduce-scatter.3.cloned.1.call-start = ((), (), s32[]{:S(2)}) async-start(), calls=%async_computation.3 | async-start | bytes 14155776 | tf_op jit(solution)/shard_map/reduce_scatter | solution.py:30
  58.5 1.4 copy-start
  58.5 386.9 %all-gather.5.cloned.1.call-start = ((), (), s32[]{:S(2)}) async-start(), calls=%async_computation.4 | async-start | bytes 14155776 | tf_op jit(solution)/shard_map/all_gather | solution.py:37
  60.2 7.8 %collective-permute-start.6 = (f32[512]{0:T(512)S(1)}, f32[512]{0:T(512)S(1)}, u32[]{:S(2)}, u32[]{:S(2)}) collective-permute-start(f32[512]{0:T(512)S(1)} %fusion.1), channel_id=1, source_target_pairs={{0,28},{4,0},{8,4},{12,8},{16,12},{20,16},{24,20},{28,24},{1,29},{... | collective-permute-start | bytes 6152 | tf_op jit(solution)/shard_map/ppermute | solution.py:20
  64.5 5.5 %collective-permute-start.5 = (f32[512]{0:T(512)S(1)}, f32[512]{0:T(512)S(1)}, u32[]{:S(2)}, u32[]{:S(2)}) collective-permute-start(f32[512]{0:T(512)S(1)} %fusion.1), channel_id=1, source_target_pairs={{0,24},{4,28},{8,0},{12,4},{16,8},{20,12},{24,16},{28,20},{1,25},{... | collective-permute-start | bytes 6152 | tf_op jit(solution)/shard_map/ppermute | solution.py:20
  65.1 5.9 %collective-permute-start.4 = (f32[512]{0:T(512)S(1)}, f32[512]{0:T(512)S(1)}, u32[]{:S(2)}, u32[]{:S(2)}) collective-permute-start(f32[512]{0:T(512)S(1)} %fusion.1), channel_id=1, source_target_pairs={{0,20},{4,24},{8,28},{12,0},{16,4},{20,8},{24,12},{28,16},{1,21},{... | collective-permute-start | bytes 6152 | tf_op jit(solution)/shard_map/ppermute | solution.py:20
  65.1 5.9 %collective-permute-start.3 = (f32[512]{0:T(512)S(1)}, f32[512]{0:T(512)S(1)}, u32[]{:S(2)}, u32[]{:S(2)}) collective-permute-start(f32[512]{0:T(512)S(1)} %fusion.1), channel_id=1, source_target_pairs={{0,16},{4,20},{8,24},{12,28},{16,0},{20,4},{24,8},{28,12},{1,17},{... | collective-permute-start | bytes 6152 | tf_op jit(solution)/shard_map/ppermute | solution.py:20
  68.0 5.6 %collective-permute-start.2 = (f32[512]{0:T(512)S(1)}, f32[512]{0:T(512)S(1)}, u32[]{:S(2)}, u32[]{:S(2)}) collective-permute-start(f32[512]{0:T(512)S(1)} %fusion.1), channel_id=1, source_target_pairs={{0,12},{4,16},{8,20},{12,24},{16,28},{20,0},{24,4},{28,8},{1,13},{... | collective-permute-start | bytes 6152 | tf_op jit(solution)/shard_map/ppermute | solution.py:20
  68.0 6.6 %collective-permute-start.1 = (f32[512]{0:T(512)S(1)}, f32[512]{0:T(512)S(1)}, u32[]{:S(2)}, u32[]{:S(2)}) collective-permute-start(f32[512]{0:T(512)S(1)} %fusion.1), channel_id=1, source_target_pairs={{0,8},{4,12},{8,16},{12,20},{16,24},{20,28},{24,0},{28,4},{1,9},{5... | collective-permute-start | bytes 6152 | tf_op jit(solution)/shard_map/ppermute | solution.py:20
  70.0 6.5 %collective-permute-start = (f32[512]{0:T(512)S(1)}, f32[512]{0:T(512)S(1)}, u32[]{:S(2)}, u32[]{:S(2)}) collective-permute-start(f32[512]{0:T(512)S(1)} %fusion.1), channel_id=1, source_target_pairs={{0,4},{4,8},{8,12},{12,16},{16,20},{20,24},{24,28},{28,0},{1,5},{5... | collective-permute-start | bytes 6152 | tf_op jit(solution)/shard_map/ppermute | solution.py:20
  270.0 229.0 %copy-start.1 = (bf16[128,1536]{1,0:T(8,128)(2,1)S(1)}, bf16[128,1536]{1,0:T(8,128)(2,1)}, u32[]{:S(2)}) copy-start(bf16[128,1536]{1,0:T(8,128)(2,1)} %param.4) | copy-start | bytes 1179652
  270.1 229.0 %reduce-scatter.5.cloned.1.call-start = ((), (), s32[]{:S(2)}) async-start(), calls=%async_computation.5 | async-start | bytes 1966080 | tf_op jit(solution)/shard_map/reduce_scatter | solution.py:41
Sparse Core Ops, SparseCore 0:
  8.9 22.3 all-gather.2
  58.6 207.5 reduce-scatter.2
  270.2 175.2 all-gather.4
  472.7 26.2 reduce-scatter.4
